TPU v7x, 32 devices: a whole 2x2x4 slice. The times are simulated.
32 devices in a mesh: dp: 8 (over y, x, core), tensor: 4 (over z).
Axes of the slice: x: 2, y: 2, z: 4, core: 2. Of those that a mesh axis runs over, the one named last changes fastest.
Arguments:
- tokens: bfloat16 [16, 320, 1536], P('dp', 'tensor'), may hold values from -6 to 6
- cotangent: bfloat16 [16, 320, 1536], P('dp', 'tensor'), may hold values from -6 to 6
- order: int32 [16, 320], P('dp'), may hold values from 0 to 319, each once within a row
- lengths: int32 [16, 3], P('dp'), may hold values from 1 to 256, 320 in all within a row
- gain_attn: bfloat16 [1536], P('dp'), may hold values from 0.5 to 1.5
- w_query: bfloat16 [1536, 1536], P('dp', 'tensor'), may hold values from -0.15625 to 0.15625
- w_key: bfloat16 [1536, 768], P('dp', 'tensor'), may hold values from -0.15625 to 0.15625
- w_value: bfloat16 [1536, 768], P('dp', 'tensor'), may hold values from -0.15625 to 0.15625
- w_out: bfloat16 [1536, 1536], P('tensor', 'dp'), may hold values from -1.5 to 1.5
- gain_ffn: bfloat16 [1536], P('dp'), may hold values from 0.5 to 1.5
- w_gate: bfloat16 [1536, 4096], P('dp', 'tensor'), may hold values from -0.15625 to 0.15625
- w_up: bfloat16 [1536, 4096], P('dp', 'tensor'), may hold values from -0.15625 to 0.15625
- w_down: bfloat16 [4096, 1536], P('tensor', 'dp'), may hold values from -0.09375 to 0.09375
Outputs:
- output: bfloat16 [16, 320, 1536], P('dp', 'tensor')
- grad_tokens: float32 [16, 320, 1536], P('dp', 'tensor')
- grad_gain_attn: float32 [1536], P('dp')
- grad_query: float32 [1536, 1536], P('dp', 'tensor')
- grad_key: float32 [1536, 768], P('dp', 'tensor')
- grad_value: float32 [1536, 768], P('dp', 'tensor')
- grad_out: float32 [1536, 1536], P('tensor', 'dp')
- grad_gain_ffn: float32 [1536], P('dp')
- grad_gate: float32 [1536, 4096], P('dp', 'tensor')
- grad_up: float32 [1536, 4096], P('dp', 'tensor')
- grad_down: float32 [4096, 1536], P('tensor', 'dp')
Inputs may be any that keep to these rules, and one draw needn't show every extreme that they name: `order`: each row is a permutation of 0 to 319. `lengths`: each row sums to 320; its largest entry is 256; the last document of each stream is padding.
All inputs are finite; a program needn't handle non-finite values.
Results may differ from a plain program's by a relative error of at most 0.012.
Values may be sent and summed in bfloat16 or wider, within the bound.
A program may use at most 128 MiB of HBM per device.

v0:
```python
import jax
import jax.numpy as jnp
from jax import lax
from jax.sharding import PartitionSpec as P

HEAD = 96
eps = 1e-05
rope_base = 100000.0


def rotate(field, cosine, sine):
    half = field.shape[-1] // 2
    first = field[..., :half]
    second = field[..., half:]
    return jnp.concatenate(
        [first * cosine - second * sine, second * cosine + first * sine], axis=-1
    )


def rotate_back(field, cosine, sine):
    half = field.shape[-1] // 2
    first = field[..., :half]
    second = field[..., half:]
    return jnp.concatenate(
        [first * cosine + second * sine, second * cosine - first * sine], axis=-1
    )


def layout(order, lengths):
    starts = jnp.cumsum(lengths, dtype=jnp.int32) - lengths
    docs = jnp.sum((order[:, None] >= starts[None, 1:]).astype(jnp.int32), axis=1, dtype=jnp.int32)
    onehot = docs[:, None] == jnp.arange(lengths.shape[0], dtype=jnp.int32)[None, :]
    first = jnp.sum(jnp.where(onehot, starts[None, :], 0), axis=1, dtype=jnp.int32)
    positions = (order - first).astype(jnp.float32)
    mask = (docs[:, None] == docs[None, :]) & (order[None, :] <= order[:, None])
    real = (docs < lengths.shape[0] - 1).astype(jnp.float32)
    return (positions, mask, real)


def norm_forward(rows, gain):
    scale = lax.rsqrt(jnp.mean(rows * rows, axis=-1, keepdims=True) + eps)
    unit = rows * scale
    return (unit, scale, (unit * gain).astype(jnp.bfloat16))


def norm_backward(grad, unit, scale, gain):
    inner = grad * gain
    return scale * (inner - unit * jnp.mean(inner * unit, axis=-1, keepdims=True))


def contract_rows(left, right):
    return lax.dot_general(
        left, right, (((0,), (0,)), ((), ())), preferred_element_type=jnp.float32
    )


def times_transpose(left, right):
    return lax.dot_general(
        left, right, (((1,), (1,)), ((), ())), preferred_element_type=jnp.float32
    )


def gather_weights(gain_attn, w_query, w_key, w_value, w_out, gain_ffn, w_gate, w_up, w_down):
    gains = lax.all_gather(jnp.stack([gain_attn, gain_ffn], axis=0), "dp", axis=1, tiled=True)
    attn = lax.all_gather(
        jnp.concatenate([w_query, w_key, w_value, w_out.T], axis=1), "dp", axis=0, tiled=True
    )
    gate_up = lax.all_gather(jnp.concatenate([w_gate, w_up], axis=1), "dp", axis=0, tiled=True)
    down = lax.all_gather(w_down.T, "dp", axis=0, tiled=True)
    return (gains, attn, gate_up, down)


def gather_rows(rows):
    return lax.all_gather(rows, "tensor", axis=1, tiled=True)


def scatter_rows(partial):
    low = partial.astype(jnp.bfloat16)
    return lax.psum_scatter(low, "tensor", scatter_dimension=1, tiled=True).astype(jnp.float32)


def reduce_weights(term):
    low = term.astype(jnp.bfloat16)
    return lax.psum_scatter(low, "dp", scatter_dimension=0, tiled=True).astype(jnp.float32)


def local(
    tokens,
    cotangent,
    order,
    lengths,
    gain_attn,
    w_query,
    w_key,
    w_value,
    w_out,
    gain_ffn,
    w_gate,
    w_up,
    w_down,
):
    micro, rows, width = tokens.shape
    seq = rows * lax.axis_size("tensor")
    q_cols, k_cols, ff_cols = (w_query.shape[1], w_key.shape[1], w_gate.shape[1])
    local_heads, local_kv = (q_cols // HEAD, k_cols // HEAD)
    group = local_heads // local_kv
    first_row = lax.axis_index("tensor") * rows
    freqs = rope_base ** (-2.0 * jnp.arange(HEAD // 2, dtype=jnp.float32) / HEAD)
    head_scale = HEAD ** (-0.5)
    gains, attn, gate_up, down = gather_weights(
        gain_attn, w_query, w_key, w_value, w_out, gain_ffn, w_gate, w_up, w_down
    )
    gain1, gain2 = (gains[0].astype(jnp.float32), gains[1].astype(jnp.float32))
    in_cols = q_cols + 2 * k_cols
    w_in, w_out_t = (attn[:, :in_cols], attn[:, in_cols:])
    positions, mask, real = jax.vmap(layout)(order, lengths)
    angles = positions[:, :, None] * freqs
    cosine, sine = (jnp.cos(angles)[:, :, None, :], jnp.sin(angles)[:, :, None, :])
    mask = mask[:, None, None]
    real_rows = lax.dynamic_slice_in_dim(real, first_row, rows, 1)[:, :, None]
    stream = tokens.astype(jnp.float32)
    unit1, scale1, normed1 = norm_forward(stream, gain1)
    full1 = gather_rows(normed1)
    grad_out_rows = cotangent.astype(jnp.float32) * real_rows
    full_grad = gather_rows(grad_out_rows.astype(jnp.bfloat16))
    flat1 = full1.reshape(micro * seq, width)
    flat_grad = full_grad.reshape(micro * seq, width)
    mixed_in = jnp.dot(flat1, w_in, preferred_element_type=jnp.float32).reshape(micro, seq, in_cols)
    query = mixed_in[..., :q_cols].reshape(micro, seq, local_heads, HEAD)
    keys = mixed_in[..., q_cols : q_cols + k_cols].reshape(micro, seq, local_kv, HEAD)
    values = (
        mixed_in[..., q_cols + k_cols :].reshape(micro, seq, local_kv, HEAD).astype(jnp.bfloat16)
    )
    query = (rotate(query, cosine, sine) * head_scale).astype(jnp.bfloat16)
    query = query.reshape(micro, seq, local_kv, group, HEAD)
    keys = rotate(keys, cosine, sine).astype(jnp.bfloat16)
    scores = jnp.einsum("bqkgd,bskd->bkgqs", query, keys, preferred_element_type=jnp.float32)
    scores = jnp.where(mask, scores, -1e30)
    peak = jnp.max(scores, axis=-1, keepdims=True)
    expon = jnp.exp(scores - peak)
    total = jnp.sum(expon, axis=-1, keepdims=True)
    probs = expon / total
    probs_low = probs.astype(jnp.bfloat16)
    mixed = jnp.einsum("bkgqs,bskd->bqkgd", probs_low, values, preferred_element_type=jnp.float32)
    mixed = mixed.reshape(micro * seq, q_cols).astype(jnp.bfloat16)
    branch = scatter_rows(times_transpose(mixed, w_out_t).reshape(micro, seq, width))
    resid = stream + branch
    unit2, scale2, normed2 = norm_forward(resid, gain2)
    full2 = gather_rows(normed2).reshape(micro * seq, width)
    both = jnp.dot(full2, gate_up, preferred_element_type=jnp.float32)
    gate, upper = (both[:, :ff_cols], both[:, ff_cols:])
    sigma = jax.nn.sigmoid(gate)
    hidden = (gate * sigma * upper).astype(jnp.bfloat16)
    ffn = scatter_rows(times_transpose(hidden, down).reshape(micro, seq, width))
    output = ((resid + ffn) * real_rows).astype(jnp.bfloat16)
    grad_hidden = jnp.dot(flat_grad, down, preferred_element_type=jnp.float32)
    grad_gate = (grad_hidden * upper * sigma * (1.0 + gate * (1.0 - sigma))).astype(jnp.bfloat16)
    grad_up = (grad_hidden * gate * sigma).astype(jnp.bfloat16)
    grad_both = jnp.concatenate([grad_gate, grad_up], axis=1)
    grad_norm2 = scatter_rows(times_transpose(grad_both, gate_up).reshape(micro, seq, width))
    final_down = reduce_weights(contract_rows(flat_grad, hidden))
    final_gate = reduce_weights(contract_rows(full2, grad_gate))
    final_up = reduce_weights(contract_rows(full2, grad_up))
    term_gain2 = jnp.sum(grad_norm2 * unit2, axis=(0, 1))
    grad_resid = grad_out_rows + norm_backward(grad_norm2, unit2, scale2, gain2)
    full_resid = gather_rows(grad_resid.astype(jnp.bfloat16)).reshape(micro * seq, width)
    grad_mixed = jnp.dot(full_resid, w_out_t, preferred_element_type=jnp.float32).astype(
        jnp.bfloat16
    )
    final_out = reduce_weights(contract_rows(full_resid, mixed))
    grad_heads = grad_mixed.reshape(micro, seq, local_kv, group, HEAD)
    grad_probs = jnp.einsum(
        "bqkgd,bskd->bkgqs", grad_heads, values, preferred_element_type=jnp.float32
    )
    grad_values = jnp.einsum(
        "bkgqs,bqkgd->bskd", probs_low, grad_heads, preferred_element_type=jnp.float32
    )
    grad_scores = (
        probs * (grad_probs - jnp.sum(probs * grad_probs, axis=-1, keepdims=True))
    ).astype(jnp.bfloat16)
    grad_query = jnp.einsum(
        "bkgqs,bskd->bqkgd", grad_scores, keys, preferred_element_type=jnp.float32
    ).reshape(micro, seq, local_heads, HEAD)
    grad_keys = jnp.einsum(
        "bkgqs,bqkgd->bskd", grad_scores, query, preferred_element_type=jnp.float32
    )
    grad_query = rotate_back(grad_query * head_scale, cosine, sine).reshape(micro * seq, q_cols)
    grad_keys = rotate_back(grad_keys, cosine, sine).reshape(micro * seq, k_cols)
    grad_values = grad_values.reshape(micro * seq, k_cols)
    grad_in = jnp.concatenate(
        [
            grad_query.astype(jnp.bfloat16),
            grad_keys.astype(jnp.bfloat16),
            grad_values.astype(jnp.bfloat16),
        ],
        axis=1,
    )
    grad_norm1 = scatter_rows(times_transpose(grad_in, w_in).reshape(micro, seq, width))
    final_in = reduce_weights(contract_rows(flat1, grad_in))
    term_gain1 = jnp.sum(grad_norm1 * unit1, axis=(0, 1))
    grad_tokens = grad_resid + norm_backward(grad_norm1, unit1, scale1, gain1)
    gain_terms = lax.psum(jnp.stack([term_gain1, term_gain2], axis=0), ("dp", "tensor"))
    own = gain_attn.shape[0]
    gain_own = lax.dynamic_slice_in_dim(gain_terms, lax.axis_index("dp") * own, own, 1)
    return (
        output,
        grad_tokens,
        gain_own[0],
        final_in[:, :q_cols],
        final_in[:, q_cols : q_cols + k_cols],
        final_in[:, q_cols + k_cols :],
        final_out.T,
        gain_own[1],
        final_gate,
        final_up,
        final_down.T,
    )


def solution(mesh):
    return jax.shard_map(
        local,
        mesh=mesh,
        in_specs=(
            P("dp", "tensor", None),
            P("dp", "tensor", None),
            P("dp", None),
            P("dp", None),
            P("dp"),
            P("dp", "tensor"),
            P("dp", "tensor"),
            P("dp", "tensor"),
            P("tensor", "dp"),
            P("dp"),
            P("dp", "tensor"),
            P("dp", "tensor"),
            P("tensor", "dp"),
        ),
        out_specs=(
            P("dp", "tensor", None),
            P("dp", "tensor", None),
            P("dp"),
            P("dp", "tensor"),
            P("dp", "tensor"),
            P("dp", "tensor"),
            P("tensor", "dp"),
            P("dp"),
            P("dp", "tensor"),
            P("dp", "tensor"),
            P("tensor", "dp"),
        ),
        check_vma=False,
    )
```

profile of v0, /device:TPU:0, one launch (start us, length us, event | category | flops | bytes accessed | tf_op | source)
XLA Modules:
  0.0 763.6 jit_solution(17415708524543095408)
XLA Ops:
  10.0 10.4 %all-gather = bf16[8,192,2]{1,2,0:T(2,128)(2,1)S(1)} all-gather(bf16[1,192,2]{1,2,0:T(2,128)(2,1)S(1)} %maximum_bitcast_fusion.8), channel_id=1, replica_groups=mesh['dp'=8,'tensor'=4] {'dp'}, dimensions={0}, use_global_device_ids=true | all-gather | bytes 6912 | tf_op jit(solution)/shard_map/all_gather | solution.py:64
  20.6 2.0 fusion.35
  25.8 40.8 %all-gather.9.cloned.1.call-done = bf16[2,320,1536]{2,1,0:T(8,128)(2,1)} async-done(((bf16[2,80,1536]{2,1,0:T(8,128)(2,1)}), bf16[2,320,1536]{2,1,0:T(8,128)(2,1)}) %all-gather.9.cloned.1.call-update) | async-done | bytes 1966096 | tf_op jit(solution)/shard_map/all_gather | solution.py:74
  66.5 35.2 %all-gather.11.cloned.1.call-done = bf16[1536,1152]{1,0:T(8,128)(2,1)} async-done(((bf16[192,1152]{1,0:T(8,128)(2,1)}), bf16[1536,1152]{1,0:T(8,128)(2,1)}) %all-gather.11.cloned.1.call-update) | async-done | bytes 3538960 | tf_op jit(solution)/shard_map/all_gather | solution.py:65
  101.7 3.9 fusion.8
  107.7 4.7 fusion.63
  112.5 2.7 convolution_convert_fusion.9
  115.2 3.9 convolution_convert_fusion.7
  120.3 40.7 %reduce-scatter.10.cloned.1.call-done = bf16[2,80,1536]{2,1,0:T(8,128)(2,1)} async-done(((bf16[2,320,1536]{2,1,0:T(8,128)(2,1)}), bf16[2,80,1536]{2,1,0:T(8,128)(2,1)}) %reduce-scatter.10.cloned.1.call-update) | async-done | bytes 491536 | tf_op jit(solution)/shard_map/reduce_scatter | solution.py:79
  162.2 2.0 multiply_convert_fusion.4
  166.6 41.2 %all-gather.15.cloned.1.call-done = bf16[1536,2048]{1,0:T(8,128)(2,1)} async-done(((bf16[192,2048]{1,0:T(8,128)(2,1)}), bf16[1536,2048]{1,0:T(8,128)(2,1)}) %all-gather.15.cloned.1.call-update) | async-done | bytes 6291472 | tf_op jit(solution)/shard_map/all_gather | solution.py:68
  207.8 45.5 %all-gather.13.cloned.1.call-done = bf16[2,320,1536]{2,1,0:T(8,128)(2,1)} async-done(((bf16[2,80,1536]{2,1,0:T(8,128)(2,1)}), bf16[2,320,1536]{2,1,0:T(8,128)(2,1)}) %all-gather.13.cloned.1.call-update) | async-done | bytes 1966096 | tf_op jit(solution)/shard_map/all_gather | solution.py:74
  253.3 10.0 %fusion.68 = f32[640,2048]{1,0:T(8,128)} fusion(bf16[640,1536]{1,0:T(8,128)(2,1)} %bitcast.147, bf16[1536,2048]{1,0:T(8,128)(2,1)} %all-gather.15.cloned.1.call-done), kind=kOutput, calls=%fused_computation.125 | convolution fusion | flops 4026531840 | bytes 13500416 | tf_op jit(solution)/shard_map/dot_general | solution.py:150
  263.3 34.4 %all-gather.19.cloned.1.call-done = bf16[2,320,1536]{2,1,0:T(8,128)(2,1)} async-done(((bf16[2,80,1536]{2,1,0:T(8,128)(2,1)}), bf16[2,320,1536]{2,1,0:T(8,128)(2,1)}) %all-gather.19.cloned.1.call-update) | async-done | bytes 1966096 | tf_op jit(solution)/shard_map/all_gather | solution.py:74
  297.6 32.9 %all-gather.17.cloned.1.call-done = bf16[1536,1024]{1,0:T(8,128)(2,1)} async-done(((bf16[192,1024]{1,0:T(8,128)(2,1)}), bf16[1536,1024]{1,0:T(8,128)(2,1)}) %all-gather.17.cloned.1.call-update) | async-done | bytes 3145744 | tf_op jit(solution)/shard_map/all_gather | solution.py:69
  330.6 8.4 %multiply_convert_fusion.1 = (bf16[640,1024]{1,0:T(8,128)(2,1)S(1)}, bf16[640,1024]{1,0:T(8,128)(2,1)S(1)}, bf16[640,1024]{1,0:T(8,128)(2,1)}) fusion(f32[640,2048]{1,0:T(8,128)} %fusion.68, bf16[640,1536]{1,0:T(8,128)(2,1)} %bitcast.150, bf16[1536,1024]{1,0:T(8,128)(2,1)} %all-gather.17.cloned.1.call-done), kind=kOutput, calls=%fused_computation.22 | convolution fusion | flops 2023751680 | bytes 14286848 | tf_op jit(solution)/shard_map/dot_general | solution.py:156
  339.0 5.5 convolution_convert_fusion.5
  344.6 41.7 %reduce-scatter.14.cloned.1.call-done = bf16[2,80,1536]{2,1,0:T(8,128)(2,1)} async-done(((bf16[2,320,1536]{2,1,0:T(8,128)(2,1)}), bf16[2,80,1536]{2,1,0:T(8,128)(2,1)}) %reduce-scatter.14.cloned.1.call-update) | async-done | bytes 491536 | tf_op jit(solution)/shard_map/reduce_scatter | solution.py:79
  386.3 1.5 fusion.34
  387.8 2.2 fusion.43
  390.1 6.2 convolution_convert_fusion.2
  396.5 6.4 convolution_convert_fusion.1
  403.0 6.3 convolution_convert_fusion
  411.2 21.6 %all-gather.21.cloned.1.call-done = bf16[2,320,1536]{2,1,0:T(8,128)(2,1)} async-done(((bf16[2,80,1536]{2,1,0:T(8,128)(2,1)}), bf16[2,320,1536]{2,1,0:T(8,128)(2,1)}) %all-gather.21.cloned.1.call-update) | async-done | bytes 1966096 | tf_op jit(solution)/shard_map/all_gather | solution.py:74
  432.8 3.0 convolution_convert_fusion.10
  437.1 2.9 fusion.23
  441.2 3.3 fusion.1
  446.5 1.6 convolution_bitcast_fusion.1
  448.5 2.5 convolution_convert_fusion.8
  453.5 1.9 convert_element_type.201
  455.4 1.7 convolution_multiply_fusion
  460.3 3.4 convolution_convert_fusion.3
  465.0 4.8 convolution_convert_fusion.4
  471.0 5.4 convolution_convert_fusion.6
  476.5 4.5 reduce-scatter.22.cloned.1.call-done
  481.0 2.0 convert_element_type.213
  482.9 47.5 %reduce-scatter.24.cloned.1.call-done = bf16[192,1024]{1,0:T(8,128)(2,1)} async-done(((bf16[1536,1024]{1,0:T(8,128)(2,1)}), bf16[192,1024]{1,0:T(8,128)(2,1)}) %reduce-scatter.24.cloned.1.call-update) | async-done | bytes 393232 | tf_op jit(solution)/shard_map/reduce_scatter | solution.py:84
  530.5 2.0 convert_element_type.215
  532.4 47.4 %reduce-scatter.26.cloned.1.call-done = bf16[192,1024]{1,0:T(8,128)(2,1)} async-done(((bf16[1536,1024]{1,0:T(8,128)(2,1)}), bf16[192,1024]{1,0:T(8,128)(2,1)}) %reduce-scatter.26.cloned.1.call-update) | async-done | bytes 393232 | tf_op jit(solution)/shard_map/reduce_scatter | solution.py:84
  579.8 2.0 convert_bitcast_fusion
  581.8 38.0 %reduce-scatter.20.cloned.1.call-done = bf16[192,384]{1,0:T(8,128)(2,1)} async-done(((bf16[1536,384]{1,0:T(8,128)(2,1)}), bf16[192,384]{1,0:T(8,128)(2,1)}) %reduce-scatter.20.cloned.1.call-update) | async-done | bytes 147472 | tf_op jit(solution)/shard_map/reduce_scatter | solution.py:84
  619.7 1.6 convert_bitcast_fusion.1
  621.4 43.9 %reduce-scatter.18.cloned.1.call-done = bf16[192,768]{1,0:T(8,128)(2,1)} async-done(((bf16[1536,768]{1,0:T(8,128)(2,1)}), bf16[192,768]{1,0:T(8,128)(2,1)}) %reduce-scatter.18.cloned.1.call-update) | async-done | bytes 294928 | tf_op jit(solution)/shard_map/reduce_scatter | solution.py:84
  665.3 1.6 slice.110
  667.0 1.7 fusion.61
  668.7 40.4 %reduce-scatter.16.cloned.1.call-done = bf16[2,80,1536]{2,1,0:T(8,128)(2,1)} async-done(((bf16[2,320,1536]{2,1,0:T(8,128)(2,1)}), bf16[2,80,1536]{2,1,0:T(8,128)(2,1)}) %reduce-scatter.16.cloned.1.call-update) | async-done | bytes 491536 | tf_op jit(solution)/shard_map/reduce_scatter | solution.py:79
  710.6 42.5 %psum.7 = f32[2,1536]{1,0:T(2,128)S(1)} all-reduce(f32[2,1536]{1,0:T(2,128)S(1)} %pad_maximum_fusion.3), channel_id=1, replica_groups=mesh['dp'=8,'tensor'=4] {'dp','tensor'}, use_global_device_ids=true, to_apply=%region_16.17 | all-reduce | flops 3072 | bytes 24576 | tf_op jit(solution)/shard_map/psum | solution.py:202
  753.7 3.1 fusion.30
  (159 shorter events, 30.1 us)
Async XLA Ops:
  7.2 15.5 %copy-start.24 = (bf16[384,192]{0,1:T(8,128)(2,1)S(1)}, bf16[384,192]{0,1:T(8,128)(2,1)}, u32[]{:S(2)}) copy-start(bf16[384,192]{0,1:T(8,128)(2,1)} %param.21) | copy-start | bytes 442372
  7.2 15.5 %copy-start.26 = (bf16[192,192]{1,0:T(8,128)(2,1)S(1)}, bf16[192,192]{1,0:T(8,128)(2,1)}, u32[]{:S(2)}) copy-start(bf16[192,192]{1,0:T(8,128)(2,1)} %param.20) | copy-start | bytes 221188
  7.2 15.5 %copy-start.25 = (bf16[192,192]{1,0:T(8,128)(2,1)S(1)}, bf16[192,192]{1,0:T(8,128)(2,1)}, u32[]{:S(2)}) copy-start(bf16[192,192]{1,0:T(8,128)(2,1)} %param.19) | copy-start | bytes 221188
  7.2 15.5 %copy-start.23 = (bf16[192,384]{1,0:T(8,128)(2,1)S(1)}, bf16[192,384]{1,0:T(8,128)(2,1)}, u32[]{:S(2)}) copy-start(bf16[192,384]{1,0:T(8,128)(2,1)} %param.18) | copy-start | bytes 442372
  7.2 16.4 %copy-start.28 = (s32[2,3]{1,0:T(2,128)S(1)}, s32[2,3]{1,0:T(2,128)}, u32[]{:S(2)}) copy-start(s32[2,3]{1,0:T(2,128)} %param.16) | copy-start | bytes 76
  7.2 16.8 %copy-start.27 = (s32[2,320]{1,0:T(2,128)S(1)}, s32[2,320]{1,0:T(2,128)}, u32[]{:S(2)}) copy-start(s32[2,320]{1,0:T(2,128)} %param.15) | copy-start | bytes 7684
  7.2 59.3 %all-gather.9.cloned.1.call-start = ((), (), s32[]{:S(2)}) async-start(), calls=%async_computation.9 | async-start | bytes 2457600 | tf_op jit(solution)/shard_map/all_gather | solution.py:74
  22.6 79.1 %all-gather.11.cloned.1.call-start = ((), (), s32[]{:S(2)}) async-start(), calls=%async_computation.10 | async-start | bytes 3981312 | tf_op jit(solution)/shard_map/all_gather | solution.py:65
  23.6 137.3 %reduce-scatter.10.cloned.1.call-start = ((), (), s32[]{:S(2)}) async-start(), calls=%async_computation.11 | async-start | bytes 2457600 | tf_op jit(solution)/shard_map/reduce_scatter | solution.py:79
  25.8 81.8 %copy-start.5 = (f32[2,320,48]{1,2,0:T(8,128)}, f32[2,320,48]{1,2,0:T(8,128)S(1)}, u32[]{:S(2)}) copy-start(f32[2,320,48]{1,2,0:T(8,128)S(1)} %get-tuple-element.34) | copy-start | bytes 368644
  25.8 81.8 %copy-start.7 = (f32[2,320,48]{1,2,0:T(8,128)}, f32[2,320,48]{1,2,0:T(8,128)S(1)}, u32[]{:S(2)}) copy-start(f32[2,320,48]{1,2,0:T(8,128)S(1)} %get-tuple-element.35) | copy-start | bytes 368644
  107.5 5.0 copy-start.15
  107.5 4.9 copy-start.16
  107.7 4.8 copy-start.9
  107.7 4.8 copy-start.11
  107.7 4.8 copy-start.20
  115.2 4.0 copy-start.18
  115.2 4.0 copy-start.19
  119.1 41.8 %copy-start = (bf16[2,80,1536]{2,1,0:T(8,128)(2,1)S(1)}, bf16[2,80,1536]{2,1,0:T(8,128)(2,1)}, u32[]{:S(2)}) copy-start(bf16[2,80,1536]{2,1,0:T(8,128)(2,1)} %param.13) | copy-start | bytes 1474564
  119.2 88.6 %all-gather.15.cloned.1.call-start = ((), (), s32[]{:S(2)}) async-start(), calls=%async_computation.13 | async-start | bytes 7077888 | tf_op jit(solution)/shard_map/all_gather | solution.py:68
  120.2 44.2 %copy-start.2 = (bf16[2,80,1536]{2,1,0:T(8,128)(2,1)S(1)}, bf16[2,80,1536]{2,1,0:T(8,128)(2,1)}, u32[]{:S(2)}) copy-start(bf16[2,80,1536]{2,1,0:T(8,128)(2,1)} %param.14) | copy-start | bytes 1474564
  120.2 133.1 %all-gather.13.cloned.1.call-start = ((), (), s32[]{:S(2)}) async-start(), calls=%async_computation.12 | async-start | bytes 2457600 | tf_op jit(solution)/shard_map/all_gather | solution.py:74
  164.2 133.4 %all-gather.19.cloned.1.call-start = ((), (), s32[]{:S(2)}) async-start(), calls=%async_computation.16 | async-start | bytes 2457600 | tf_op jit(solution)/shard_map/all_gather | solution.py:74
  165.3 165.3 %all-gather.17.cloned.1.call-start = ((), (), s32[]{:S(2)}) async-start(), calls=%async_computation.14 | async-start | bytes 3538944 | tf_op jit(solution)/shard_map/all_gather | solution.py:69
  166.1 220.2 %reduce-scatter.14.cloned.1.call-start = ((), (), s32[]{:S(2)}) async-start(), calls=%async_computation.17 | async-start | bytes 2457600 | tf_op jit(solution)/shard_map/reduce_scatter | solution.py:79
  330.6 8.4 %copy-start.29 = (bf16[1536,2048]{1,0:T(8,128)(2,1)S(1)}, bf16[1536,2048]{1,0:T(8,128)(2,1)}, u32[]{:S(2)}) copy-start(bf16[1536,2048]{1,0:T(8,128)(2,1)} %all-gather.15.cloned.1.call-done) | copy-start | bytes 18874372
  339.0 5.5 copy-start.33
  339.0 5.5 copy-start.34
  344.5 41.8 %copy-start.1 = (bf16[2,80,1536]{2,1,0:T(8,128)(2,1)S(1)}, bf16[2,80,1536]{2,1,0:T(8,128)(2,1)}, u32[]{:S(2)}) copy-start(bf16[2,80,1536]{2,1,0:T(8,128)(2,1)} %reduce-scatter.10.cloned.1.call-done) | copy-start | bytes 1474564
  344.5 88.3 %all-gather.21.cloned.1.call-start = ((), (), s32[]{:S(2)}) async-start(), calls=%async_computation.18 | async-start | bytes 2457600 | tf_op jit(solution)/shard_map/all_gather | solution.py:74
  390.0 90.9 %reduce-scatter.22.cloned.1.call-start = ((), (), s32[]{:S(2)}) async-start(), calls=%async_computation.22 | async-start | bytes 3538944 | tf_op jit(solution)/shard_map/reduce_scatter | solution.py:84
  396.3 134.2 %reduce-scatter.24.cloned.1.call-start = ((), (), s32[]{:S(2)}) async-start(), calls=%async_computation.23 | async-start | bytes 3538944 | tf_op jit(solution)/shard_map/reduce_scatter | solution.py:84
  402.9 176.9 %reduce-scatter.26.cloned.1.call-start = ((), (), s32[]{:S(2)}) async-start(), calls=%async_computation.24 | async-start | bytes 3538944 | tf_op jit(solution)/shard_map/reduce_scatter | solution.py:84
  409.3 210.4 %reduce-scatter.20.cloned.1.call-start = ((), (), s32[]{:S(2)}) async-start(), calls=%async_computation.21 | async-start | bytes 1327104 | tf_op jit(solution)/shard_map/reduce_scatter | solution.py:84
  441.2 3.9 copy-start.4
  445.1 1.3 copy-start.12
  446.5 1.6 copy-start.17
  446.5 2.0 copy-start.31
  451.0 214.3 %reduce-scatter.18.cloned.1.call-start = ((), (), s32[]{:S(2)}) async-start(), calls=%async_computation.20 | async-start | bytes 2654208 | tf_op jit(solution)/shard_map/reduce_scatter | solution.py:84
  455.4 1.7 copy-start.6
  455.4 1.7 copy-start.8
  457.2 1.2 copy-start.14
  458.4 1.9 copy-start.30
  463.7 1.2 copy-start.22
  463.8 245.3 %reduce-scatter.16.cloned.1.call-start = ((), (), s32[]{:S(2)}) async-start(), calls=%async_computation.19 | async-start | bytes 2457600 | tf_op jit(solution)/shard_map/reduce_scatter | solution.py:79
  469.7 1.3 copy-start.32
  469.8 284.0 %reduce-scatter.12.cloned.1.call-start = ((), (), s32[]{:S(2)}) async-start(), calls=%async_computation.15 | async-start | bytes 2457600 | tf_op jit(solution)/shard_map/reduce_scatter | solution.py:79
  532.4 221.3 %copy-start.3 = (bf16[2,80,1536]{2,1,0:T(8,128)(2,1)S(1)}, bf16[2,80,1536]{2,1,0:T(8,128)(2,1)}, u32[]{:S(2)}) copy-start(bf16[2,80,1536]{2,1,0:T(8,128)(2,1)} %reduce-scatter.14.cloned.1.call-done) | copy-start | bytes 1474564
  (3 other events, 3.2 us)
Sparse Core Ops, SparseCore 0:
  22.7 43.7 all-gather.8
  69.0 32.6 all-gather.10
  119.3 41.5 reduce-scatter.9
  163.2 44.4 all-gather.14
  209.8 43.4 all-gather.12
  255.3 42.3 all-gather.18
  299.5 31.0 all-gather.16
  344.6 41.5 reduce-scatter.13
  390.1 42.6 all-gather.20
  436.0 44.8 reduce-scatter.21
  484.3 46.0 reduce-scatter.23
  533.7 46.0 reduce-scatter.25
  583.0 36.6 reduce-scatter.19
  622.9 42.3 reduce-scatter.17
  667.5 41.5 reduce-scatter.15
  711.3 41.7 reduce-scatter.11
where the time goes:
time: 771 us; the launch traced here: 764 us
  waiting for transfers between devices  557 us (72%)
  matrix products  86.6 us (11%)
  blocking collectives  52.9 us (7%)
  other arithmetic  28.6 us (4%)
  local copies, waits for them, and re-layouts  22.7 us (3%)
  between operations  14.8 us (2%)
    reduce_scatter x5, waiting for transfers between devices, reduce_weights(): lax.psum_scatter(low, 'dp', scatter_dimension=0, tiled=True)  181 us
    all_gather x4, waiting for transfers between devices, gather_rows(): return lax.all_gather(rows, 'tensor', axis=1, tiled=True)  142 us
    reduce_scatter x4, waiting for transfers between devices, scatter_rows(): lax.psum_scatter(low, 'tensor', scatter_dimension=1, tiled=True)  123 us
    psum x1, blocking collectives, local(): lax.psum(jnp.stack([term_gain1, term_gain2], axis=0), ('dp', 'tensor'))  42.5 us
    all_gather x1, waiting for transfers between devices, gather_weights(): lax.all_gather(jnp.concatenate([w_gate, w_up], axis=1), 'dp', axis=0, til...  41.2 us
    all_gather x1, waiting for transfers between devices, gather_weights(): lax.all_gather(jnp.concatenate([w_query, w_key, w_value, w_out.T], axis=1...  35.2 us
    all_gather x1, waiting for transfers between devices, gather_weights(): down = lax.all_gather(w_down.T, 'dp', axis=0, tiled=True)  32.9 us
    dot_general x5, matrix products, contract_rows(): lax.dot_general(left, right, (((0,), (0,)), ((), ())), preferred_element_...  24.8 us
  transfers between devices with their start and end apart: 16, of which 15 were waited for; matrix products, arithmetic and copies ran while one was open for 12% of the time, Pallas kernels for 0%

commit v1 on v0

--- a/solution.py
+++ b/solution.py
@@ -199,7 +199,9 @@
     final_in = reduce_weights(contract_rows(flat1, grad_in))
     term_gain1 = jnp.sum(grad_norm1 * unit1, axis=(0, 1))
     grad_tokens = grad_resid + norm_backward(grad_norm1, unit1, scale1, gain1)
-    gain_terms = lax.psum(jnp.stack([term_gain1, term_gain2], axis=0), ("dp", "tensor"))
+    gain_terms = jnp.sum(
+        lax.all_gather(jnp.stack([term_gain1, term_gain2], axis=0), ("dp", "tensor")), axis=0
+    )
     own = gain_attn.shape[0]
     gain_own = lax.dynamic_slice_in_dim(gain_terms, lax.axis_index("dp") * own, own, 1)
     return (

time: 771 us -> 802 us (1.040)
  blocking collectives: 52.9 us -> 83.9 us
    all_gather x0 -> x1, blocking collectives: none -> 73.5 us  [local(): lax.all_gather(jnp.stack([term_gain1, term_gain2], axis=0), ('dp', 'tenso...]
    psum x1 -> x0, blocking collectives: 42.5 us -> none  [local(): lax.psum(jnp.stack([term_gain1, term_gain2], axis=0), ('dp', 'tensor'))]
  transfers between devices with their start and end apart: 16 -> 16, of which waited for: 15 -> 15; matrix products, arithmetic and copies ran while one was open for 12% -> 11% of each run, Pallas kernels for 0% -> 0%
where the time goes in v1:
time: 802 us; the launch traced here: 795 us
  waiting for transfers between devices  557 us (69%)
  matrix products  86.5 us (11%)
  blocking collectives  83.9 us (10%)
  other arithmetic  28.6 us (4%)
  local copies, waits for them, and re-layouts  22.7 us (3%)
  between operations  14.8 us (2%)
    reduce_scatter x5, waiting for transfers between devices, reduce_weights(): lax.psum_scatter(low, 'dp', scatter_dimension=0, tiled=True)  181 us
    all_gather x4, waiting for transfers between devices, gather_rows(): return lax.all_gather(rows, 'tensor', axis=1, tiled=True)  142 us
    reduce_scatter x4, waiting for transfers between devices, scatter_rows(): lax.psum_scatter(low, 'tensor', scatter_dimension=1, tiled=True)  123 us
    all_gather x1, blocking collectives, local(): lax.all_gather(jnp.stack([term_gain1, term_gain2], axis=0), ('dp', 'tenso...  73.5 us
    all_gather x1, waiting for transfers between devices, gather_weights(): lax.all_gather(jnp.concatenate([w_gate, w_up], axis=1), 'dp', axis=0, til...  41.2 us
    all_gather x1, waiting for transfers between devices, gather_weights(): lax.all_gather(jnp.concatenate([w_query, w_key, w_value, w_out.T], axis=1...  35.2 us
    all_gather x1, waiting for transfers between devices, gather_weights(): down = lax.all_gather(w_down.T, 'dp', axis=0, tiled=True)  32.9 us
    dot_general x5, matrix products, contract_rows(): lax.dot_general(left, right, (((0,), (0,)), ((), ())), preferred_element_...  24.8 us
  transfers between devices with their start and end apart: 16, of which 15 were waited for; matrix products, arithmetic and copies ran while one was open for 11% of the time, Pallas kernels for 0%

profile of v1, /device:TPU:0, one launch (start us, length us, event | category | flops | bytes accessed | tf_op | source)
XLA Modules:
  0.0 794.7 jit_solution(8344042941608497038)
XLA Ops:
  10.0 10.4 %all-gather.1 = bf16[8,192,2]{1,2,0:T(2,128)(2,1)S(1)} all-gather(bf16[1,192,2]{1,2,0:T(2,128)(2,1)S(1)} %maximum_bitcast_fusion.9), channel_id=1, replica_groups=mesh['dp'=8,'tensor'=4] {'dp'}, dimensions={0}, use_global_device_ids=true | all-gather | bytes 6912 | tf_op jit(solution)/shard_map/all_gather | solution.py:64
  20.6 2.0 fusion.35
  25.8 40.8 %all-gather.11.cloned.1.call-done = bf16[2,320,1536]{2,1,0:T(8,128)(2,1)} async-done(((bf16[2,80,1536]{2,1,0:T(8,128)(2,1)}), bf16[2,320,1536]{2,1,0:T(8,128)(2,1)}) %all-gather.11.cloned.1.call-update) | async-done | bytes 1966096 | tf_op jit(solution)/shard_map/all_gather | solution.py:74
  66.5 35.2 %all-gather.13.cloned.1.call-done = bf16[1536,1152]{1,0:T(8,128)(2,1)} async-done(((bf16[192,1152]{1,0:T(8,128)(2,1)}), bf16[1536,1152]{1,0:T(8,128)(2,1)}) %all-gather.13.cloned.1.call-update) | async-done | bytes 3538960 | tf_op jit(solution)/shard_map/all_gather | solution.py:65
  101.7 3.9 fusion.8
  107.7 4.7 fusion.63
  112.5 2.7 convolution_convert_fusion.9
  115.3 3.9 convolution_convert_fusion.7
  120.3 40.7 %reduce-scatter.10.cloned.1.call-done = bf16[2,80,1536]{2,1,0:T(8,128)(2,1)} async-done(((bf16[2,320,1536]{2,1,0:T(8,128)(2,1)}), bf16[2,80,1536]{2,1,0:T(8,128)(2,1)}) %reduce-scatter.10.cloned.1.call-update) | async-done | bytes 491536 | tf_op jit(solution)/shard_map/reduce_scatter | solution.py:79
  162.2 2.0 multiply_convert_fusion.4
  166.6 41.2 %all-gather.17.cloned.1.call-done = bf16[1536,2048]{1,0:T(8,128)(2,1)} async-done(((bf16[192,2048]{1,0:T(8,128)(2,1)}), bf16[1536,2048]{1,0:T(8,128)(2,1)}) %all-gather.17.cloned.1.call-update) | async-done | bytes 6291472 | tf_op jit(solution)/shard_map/all_gather | solution.py:68
  207.8 45.5 %all-gather.15.cloned.1.call-done = bf16[2,320,1536]{2,1,0:T(8,128)(2,1)} async-done(((bf16[2,80,1536]{2,1,0:T(8,128)(2,1)}), bf16[2,320,1536]{2,1,0:T(8,128)(2,1)}) %all-gather.15.cloned.1.call-update) | async-done | bytes 1966096 | tf_op jit(solution)/shard_map/all_gather | solution.py:74
  253.3 10.0 %fusion.68 = f32[640,2048]{1,0:T(8,128)} fusion(bf16[640,1536]{1,0:T(8,128)(2,1)} %bitcast.149, bf16[1536,2048]{1,0:T(8,128)(2,1)} %all-gather.17.cloned.1.call-done), kind=kOutput, calls=%fused_computation.125 | convolution fusion | flops 4026531840 | bytes 13500416 | tf_op jit(solution)/shard_map/dot_general | solution.py:150
  263.3 34.4 %all-gather.21.cloned.1.call-done = bf16[2,320,1536]{2,1,0:T(8,128)(2,1)} async-done(((bf16[2,80,1536]{2,1,0:T(8,128)(2,1)}), bf16[2,320,1536]{2,1,0:T(8,128)(2,1)}) %all-gather.21.cloned.1.call-update) | async-done | bytes 1966096 | tf_op jit(solution)/shard_map/all_gather | solution.py:74
  297.7 32.9 %all-gather.19.cloned.1.call-done = bf16[1536,1024]{1,0:T(8,128)(2,1)} async-done(((bf16[192,1024]{1,0:T(8,128)(2,1)}), bf16[1536,1024]{1,0:T(8,128)(2,1)}) %all-gather.19.cloned.1.call-update) | async-done | bytes 3145744 | tf_op jit(solution)/shard_map/all_gather | solution.py:69
  330.6 8.4 %multiply_convert_fusion.1 = (bf16[640,1024]{1,0:T(8,128)(2,1)S(1)}, bf16[640,1024]{1,0:T(8,128)(2,1)S(1)}, bf16[640,1024]{1,0:T(8,128)(2,1)}) fusion(f32[640,2048]{1,0:T(8,128)} %fusion.68, bf16[640,1536]{1,0:T(8,128)(2,1)} %bitcast.152, bf16[1536,1024]{1,0:T(8,128)(2,1)} %all-gather.19.cloned.1.call-done), kind=kOutput, calls=%fused_computation.22 | convolution fusion | flops 2023751680 | bytes 14286848 | tf_op jit(solution)/shard_map/dot_general | solution.py:156
  339.0 5.5 convolution_convert_fusion.5
  344.6 41.7 %reduce-scatter.14.cloned.1.call-done = bf16[2,80,1536]{2,1,0:T(8,128)(2,1)} async-done(((bf16[2,320,1536]{2,1,0:T(8,128)(2,1)}), bf16[2,80,1536]{2,1,0:T(8,128)(2,1)}) %reduce-scatter.14.cloned.1.call-update) | async-done | bytes 491536 | tf_op jit(solution)/shard_map/reduce_scatter | solution.py:79
  387.8 2.2 fusion.43
  390.1 6.2 convolution_convert_fusion.2
  396.5 6.4 convolution_convert_fusion.1
  403.0 6.3 convolution_convert_fusion
  411.2 21.6 %all-gather.23.cloned.1.call-done = bf16[2,320,1536]{2,1,0:T(8,128)(2,1)} async-done(((bf16[2,80,1536]{2,1,0:T(8,128)(2,1)}), bf16[2,320,1536]{2,1,0:T(8,128)(2,1)}) %all-gather.23.cloned.1.call-update) | async-done | bytes 1966096 | tf_op jit(solution)/shard_map/all_gather | solution.py:74
  432.8 3.0 convolution_convert_fusion.10
  437.1 2.9 fusion.23
  441.2 3.3 fusion.1
  446.5 1.6 convolution_bitcast_fusion.1
  448.5 2.5 convolution_convert_fusion.8
  453.5 1.9 convert_element_type.201
  455.4 1.6 convolution_multiply_fusion
  460.3 3.4 convolution_convert_fusion.3
  464.9 4.8 convolution_convert_fusion.4
  471.0 5.4 convolution_convert_fusion.6
  476.5 4.5 reduce-scatter.22.cloned.1.call-done
  481.0 2.0 convert_element_type.213
  482.9 47.5 %reduce-scatter.24.cloned.1.call-done = bf16[192,1024]{1,0:T(8,128)(2,1)} async-done(((bf16[1536,1024]{1,0:T(8,128)(2,1)}), bf16[192,1024]{1,0:T(8,128)(2,1)}) %reduce-scatter.24.cloned.1.call-update) | async-done | bytes 393232 | tf_op jit(solution)/shard_map/reduce_scatter | solution.py:84
  530.5 2.0 convert_element_type.215
  532.4 47.4 %reduce-scatter.26.cloned.1.call-done = bf16[192,1024]{1,0:T(8,128)(2,1)} async-done(((bf16[1536,1024]{1,0:T(8,128)(2,1)}), bf16[192,1024]{1,0:T(8,128)(2,1)}) %reduce-scatter.26.cloned.1.call-update) | async-done | bytes 393232 | tf_op jit(solution)/shard_map/reduce_scatter | solution.py:84
  579.8 2.0 convert_bitcast_fusion
  581.8 38.0 %reduce-scatter.20.cloned.1.call-done = bf16[192,384]{1,0:T(8,128)(2,1)} async-done(((bf16[1536,384]{1,0:T(8,128)(2,1)}), bf16[192,384]{1,0:T(8,128)(2,1)}) %reduce-scatter.20.cloned.1.call-update) | async-done | bytes 147472 | tf_op jit(solution)/shard_map/reduce_scatter | solution.py:84
  619.7 1.6 convert_bitcast_fusion.1
  621.4 43.9 %reduce-scatter.18.cloned.1.call-done = bf16[192,768]{1,0:T(8,128)(2,1)} async-done(((bf16[1536,768]{1,0:T(8,128)(2,1)}), bf16[192,768]{1,0:T(8,128)(2,1)}) %reduce-scatter.18.cloned.1.call-update) | async-done | bytes 294928 | tf_op jit(solution)/shard_map/reduce_scatter | solution.py:84
  665.3 1.6 slice.110
  667.0 1.7 fusion.61
  668.7 40.4 %reduce-scatter.16.cloned.1.call-done = bf16[2,80,1536]{2,1,0:T(8,128)(2,1)} async-done(((bf16[2,320,1536]{2,1,0:T(8,128)(2,1)}), bf16[2,80,1536]{2,1,0:T(8,128)(2,1)}) %reduce-scatter.16.cloned.1.call-update) | async-done | bytes 491536 | tf_op jit(solution)/shard_map/reduce_scatter | solution.py:79
  709.1 1.5 fusion.37
  710.7 73.5 %all-gather.2 = f32[32,2,1536]{2,1,0:T(2,128)S(1)} all-gather(f32[1,2,1536]{2,1,0:T(2,128)S(1)} %maximum_bitcast_fusion.8), channel_id=2, replica_groups=mesh['dp'=8,'tensor'=4] {'dp','tensor'}, dimensions={0}, use_global_device_ids=true | all-gather | bytes 405504 | tf_op jit(solution)/shard_map/all_gather | solution.py:203
  785.0 3.0 fusion.30
  (162 shorter events, 30.3 us)
Async XLA Ops:
  7.2 15.5 %copy-start.25 = (bf16[384,192]{0,1:T(8,128)(2,1)S(1)}, bf16[384,192]{0,1:T(8,128)(2,1)}, u32[]{:S(2)}) copy-start(bf16[384,192]{0,1:T(8,128)(2,1)} %param.21) | copy-start | bytes 442372
  7.2 15.5 %copy-start.27 = (bf16[192,192]{1,0:T(8,128)(2,1)S(1)}, bf16[192,192]{1,0:T(8,128)(2,1)}, u32[]{:S(2)}) copy-start(bf16[192,192]{1,0:T(8,128)(2,1)} %param.20) | copy-start | bytes 221188
  7.2 15.5 %copy-start.26 = (bf16[192,192]{1,0:T(8,128)(2,1)S(1)}, bf16[192,192]{1,0:T(8,128)(2,1)}, u32[]{:S(2)}) copy-start(bf16[192,192]{1,0:T(8,128)(2,1)} %param.19) | copy-start | bytes 221188
  7.2 15.5 %copy-start.24 = (bf16[192,384]{1,0:T(8,128)(2,1)S(1)}, bf16[192,384]{1,0:T(8,128)(2,1)}, u32[]{:S(2)}) copy-start(bf16[192,384]{1,0:T(8,128)(2,1)} %param.18) | copy-start | bytes 442372
  7.2 16.4 %copy-start.29 = (s32[2,3]{1,0:T(2,128)S(1)}, s32[2,3]{1,0:T(2,128)}, u32[]{:S(2)}) copy-start(s32[2,3]{1,0:T(2,128)} %param.16) | copy-start | bytes 76
  7.2 16.8 %copy-start.28 = (s32[2,320]{1,0:T(2,128)S(1)}, s32[2,320]{1,0:T(2,128)}, u32[]{:S(2)}) copy-start(s32[2,320]{1,0:T(2,128)} %param.15) | copy-start | bytes 7684
  7.2 59.3 %all-gather.11.cloned.1.call-start = ((), (), s32[]{:S(2)}) async-start(), calls=%async_computation.9 | async-start | bytes 2457600 | tf_op jit(solution)/shard_map/all_gather | solution.py:74
  22.6 79.1 %all-gather.13.cloned.1.call-start = ((), (), s32[]{:S(2)}) async-start(), calls=%async_computation.10 | async-start | bytes 3981312 | tf_op jit(solution)/shard_map/all_gather | solution.py:65
  23.6 137.3 %reduce-scatter.10.cloned.1.call-start = ((), (), s32[]{:S(2)}) async-start(), calls=%async_computation.11 | async-start | bytes 2457600 | tf_op jit(solution)/shard_map/reduce_scatter | solution.py:79
  25.8 81.8 %copy-start.5 = (f32[2,320,48]{1,2,0:T(8,128)}, f32[2,320,48]{1,2,0:T(8,128)S(1)}, u32[]{:S(2)}) copy-start(f32[2,320,48]{1,2,0:T(8,128)S(1)} %get-tuple-element.34) | copy-start | bytes 368644
  25.8 81.8 %copy-start.7 = (f32[2,320,48]{1,2,0:T(8,128)}, f32[2,320,48]{1,2,0:T(8,128)S(1)}, u32[]{:S(2)}) copy-start(f32[2,320,48]{1,2,0:T(8,128)S(1)} %get-tuple-element.35) | copy-start | bytes 368644
  107.5 5.0 copy-start.16
  107.5 5.0 copy-start.17
  107.7 4.8 copy-start.9
  107.7 4.8 copy-start.11
  107.7 4.8 copy-start.21
  115.2 4.0 copy-start.19
  115.2 4.0 copy-start.20
  119.1 41.8 %copy-start = (bf16[2,80,1536]{2,1,0:T(8,128)(2,1)S(1)}, bf16[2,80,1536]{2,1,0:T(8,128)(2,1)}, u32[]{:S(2)}) copy-start(bf16[2,80,1536]{2,1,0:T(8,128)(2,1)} %param.13) | copy-start | bytes 1474564
  119.2 88.6 %all-gather.17.cloned.1.call-start = ((), (), s32[]{:S(2)}) async-start(), calls=%async_computation.13 | async-start | bytes 7077888 | tf_op jit(solution)/shard_map/all_gather | solution.py:68
  120.2 44.2 %copy-start.2 = (bf16[2,80,1536]{2,1,0:T(8,128)(2,1)S(1)}, bf16[2,80,1536]{2,1,0:T(8,128)(2,1)}, u32[]{:S(2)}) copy-start(bf16[2,80,1536]{2,1,0:T(8,128)(2,1)} %param.14) | copy-start | bytes 1474564
  120.2 133.1 %all-gather.15.cloned.1.call-start = ((), (), s32[]{:S(2)}) async-start(), calls=%async_computation.12 | async-start | bytes 2457600 | tf_op jit(solution)/shard_map/all_gather | solution.py:74
  164.2 133.4 %all-gather.21.cloned.1.call-start = ((), (), s32[]{:S(2)}) async-start(), calls=%async_computation.16 | async-start | bytes 2457600 | tf_op jit(solution)/shard_map/all_gather | solution.py:74
  165.3 165.3 %all-gather.19.cloned.1.call-start = ((), (), s32[]{:S(2)}) async-start(), calls=%async_computation.14 | async-start | bytes 3538944 | tf_op jit(solution)/shard_map/all_gather | solution.py:69
  166.1 220.2 %reduce-scatter.14.cloned.1.call-start = ((), (), s32[]{:S(2)}) async-start(), calls=%async_computation.17 | async-start | bytes 2457600 | tf_op jit(solution)/shard_map/reduce_scatter | solution.py:79
  330.6 8.4 %copy-start.30 = (bf16[1536,2048]{1,0:T(8,128)(2,1)S(1)}, bf16[1536,2048]{1,0:T(8,128)(2,1)}, u32[]{:S(2)}) copy-start(bf16[1536,2048]{1,0:T(8,128)(2,1)} %all-gather.17.cloned.1.call-done) | copy-start | bytes 18874372
  339.0 5.5 copy-start.34
  339.0 5.5 copy-start.35
  344.5 41.8 %copy-start.1 = (bf16[2,80,1536]{2,1,0:T(8,128)(2,1)S(1)}, bf16[2,80,1536]{2,1,0:T(8,128)(2,1)}, u32[]{:S(2)}) copy-start(bf16[2,80,1536]{2,1,0:T(8,128)(2,1)} %reduce-scatter.10.cloned.1.call-done) | copy-start | bytes 1474564
  344.5 88.3 %all-gather.23.cloned.1.call-start = ((), (), s32[]{:S(2)}) async-start(), calls=%async_computation.18 | async-start | bytes 2457600 | tf_op jit(solution)/shard_map/all_gather | solution.py:74
  390.0 90.9 %reduce-scatter.22.cloned.1.call-start = ((), (), s32[]{:S(2)}) async-start(), calls=%async_computation.22 | async-start | bytes 3538944 | tf_op jit(solution)/shard_map/reduce_scatter | solution.py:84
  396.3 134.2 %reduce-scatter.24.cloned.1.call-start = ((), (), s32[]{:S(2)}) async-start(), calls=%async_computation.23 | async-start | bytes 3538944 | tf_op jit(solution)/shard_map/reduce_scatter | solution.py:84
  402.9 176.9 %reduce-scatter.26.cloned.1.call-start = ((), (), s32[]{:S(2)}) async-start(), calls=%async_computation.24 | async-start | bytes 3538944 | tf_op jit(solution)/shard_map/reduce_scatter | solution.py:84
  409.3 210.4 %reduce-scatter.20.cloned.1.call-start = ((), (), s32[]{:S(2)}) async-start(), calls=%async_computation.21 | async-start | bytes 1327104 | tf_op jit(solution)/shard_map/reduce_scatter | solution.py:84
  441.2 3.9 copy-start.4
  445.1 1.3 copy-start.12
  446.5 1.6 copy-start.18
  446.5 2.0 copy-start.32
  451.0 214.3 %reduce-scatter.18.cloned.1.call-start = ((), (), s32[]{:S(2)}) async-start(), calls=%async_computation.20 | async-start | bytes 2654208 | tf_op jit(solution)/shard_map/reduce_scatter | solution.py:84
  455.4 1.6 copy-start.6
  455.4 1.7 copy-start.8
  458.4 1.9 copy-start.31
  463.7 1.2 copy-start.23
  463.7 245.4 %reduce-scatter.16.cloned.1.call-start = ((), (), s32[]{:S(2)}) async-start(), calls=%async_computation.19 | async-start | bytes 2457600 | tf_op jit(solution)/shard_map/reduce_scatter | solution.py:79
  469.7 1.3 copy-start.33
  469.7 315.2 %reduce-scatter.12.cloned.1.call-start = ((), (), s32[]{:S(2)}) async-start(), calls=%async_computation.15 | async-start | bytes 2457600 | tf_op jit(solution)/shard_map/reduce_scatter | solution.py:79
  581.8 203.2 %copy-start.3 = (bf16[2,80,1536]{2,1,0:T(8,128)(2,1)S(1)}, bf16[2,80,1536]{2,1,0:T(8,128)(2,1)}, u32[]{:S(2)}) copy-start(bf16[2,80,1536]{2,1,0:T(8,128)(2,1)} %reduce-scatter.14.cloned.1.call-done) | copy-start | bytes 1474564
  709.1 75.8 %copy-start.13 = (bf16[2,80,1536]{2,1,0:T(8,128)(2,1)S(1)}, bf16[2,80,1536]{2,1,0:T(8,128)(2,1)}, u32[]{:S(2)}) copy-start(bf16[2,80,1536]{2,1,0:T(8,128)(2,1)} %reduce-scatter.16.cloned.1.call-done) | copy-start | bytes 1474564
  (4 other events, 4.4 us)
Sparse Core Ops, SparseCore 0:
  22.7 43.7 all-gather.10
  69.0 32.6 all-gather.12
  119.3 41.5 reduce-scatter.9
  163.2 44.5 all-gather.16
  209.8 43.4 all-gather.14
  255.3 42.3 all-gather.20
  299.5 31.0 all-gather.18
  344.6 41.5 reduce-scatter.13
  390.2 42.6 all-gather.22
  436.0 44.8 reduce-scatter.21
  484.4 46.0 reduce-scatter.23
  533.7 46.0 reduce-scatter.25
  583.0 36.6 reduce-scatter.19
  622.9 42.3 reduce-scatter.17
  667.5 41.5 reduce-scatter.15
  711.3 44.6 reduce-scatter.11
